TPU v7x, 256 devices: a whole 4x4x8 slice. The times are simulated.
256 devices in a mesh: atom: 16 (over z, core), wave: 16 (over y, x).
Axes of the slice: x: 4, y: 4, z: 8, core: 2. Of those that a mesh axis runs over, the one named last changes fastest.
Arguments:
- features: bfloat16 [131072, 128], P(('atom', 'wave')), may hold values from -6 to 6
- species: int32 [131072], P(('atom', 'wave')), may hold values from 0 to 15
- coords: float32 [3, 131072], P(None, ('atom', 'wave')), may hold values from 0 to 1
- wave_index: int32 [3, 16384], P(None, 'wave'), may hold values from -16 to 16, as said below
- green: float32 [16384], P('wave'), may hold values from 8.631675e-06 to 8.6316744e-05
- embed: bfloat16 [16, 128], replicated, may hold values from -3 to 3
- w_charge: bfloat16 [128, 64], replicated, may hold values from -0.5 to 0.5
- w_feat: bfloat16 [128, 256], replicated, may hold values from -0.5 to 0.5
- w_pot: bfloat16 [64, 256], replicated, may hold values from -0.75 to 0.75
- w_out: bfloat16 [256, 128], replicated, may hold values from -0.375 to 0.375
Outputs:
- updated: bfloat16 [131072, 128], P(('atom', 'wave'))
Inputs may be any that keep to these rules, and one draw needn't show every extreme that they name: `wave_index`: the 16384 wave vectors are distinct lattice vectors, and none is zero.
All inputs are finite; a program needn't handle non-finite values.
Results may differ from a plain program's by a relative error of at most 0.0075.
Values may be sent and summed in bfloat16 or wider, within the bound.
A program may use at most 128 MiB of HBM per device.

v0:
```python
import math

import jax
import jax.numpy as jnp
from jax import lax
from jax.sharding import PartitionSpec as P

TWO_PI = 2.0 * math.pi
EPS = 1e-06
BLOCK_ROWS = 1024


def copy_for_each(array, axis):
    devices = lax.axis_size(axis)
    return lax.all_to_all(
        jnp.broadcast_to(array[None], (devices, *array.shape)), axis, 0, 0, tiled=True
    )


def laid_out(parts, dim):
    lengths = list(parts.shape[1:])
    lengths[dim] *= parts.shape[0]
    return jnp.moveaxis(parts, 0, dim).reshape(lengths)


def gather_directly(array, axis, dim):
    parts = copy_for_each(array, axis)
    return laid_out(parts, dim)


def gathered_total(array, axis):
    return lax.all_gather(array, axis).sum(0)


def split_up(array, dim, devices):
    before, after = (array.shape[:dim], array.shape[dim + 1 :])
    return jnp.moveaxis(array.reshape(*before, devices, -1, *after), dim, 0)


def sent_and_summed(array, axis, dim):
    parts = split_up(array, dim, lax.axis_size(axis))
    arrived = lax.all_to_all(parts, axis, split_axis=0, concat_axis=0, tiled=True)
    return arrived.sum(axis=0)


def phases(points, waves):
    angle = points[0][:, None] * waves[0][None, :] + points[1][:, None] * waves[1][None, :]
    angle = TWO_PI * (angle + points[2][:, None] * waves[2][None, :])
    return jnp.concatenate([jnp.cos(angle), jnp.sin(angle)], axis=1).astype(jnp.bfloat16)


def phase_tile(points, waves):
    rows = points.shape[1]
    step = math.gcd(rows, BLOCK_ROWS)
    count = rows // step
    blocks = points.reshape(3, count, step).transpose(1, 0, 2)
    tiles = lax.map(lambda block: phases(block, waves), blocks)
    return tiles.reshape(rows, 2 * waves.shape[1])


def shards(features, species, coords, wave_index, green, embed, w_charge, w_feat, w_pot, w_out):
    hidden_in = features.astype(jnp.float32)
    scale = lax.rsqrt(jnp.mean(hidden_in * hidden_in, axis=1, keepdims=True) + EPS)
    onehot = (species[:, None] == jnp.arange(embed.shape[0], dtype=jnp.int32)[None, :]).astype(
        jnp.bfloat16
    )
    mixed = hidden_in * scale + jnp.dot(onehot, embed, preferred_element_type=jnp.float32)
    mixed_b = mixed.astype(jnp.bfloat16)
    charges = jnp.dot(mixed_b, w_charge, preferred_element_type=jnp.float32).astype(jnp.bfloat16)
    block_charges = gather_directly(charges, "wave", 0)
    block_points = gather_directly(coords, "wave", 1)
    waves = wave_index.astype(jnp.float32)
    tile = phase_tile(block_points, waves)
    green_both = jnp.concatenate([green, green])
    partial_value = lax.dot_general(
        tile, block_charges, (((0,), (0,)), ((), ())), preferred_element_type=jnp.float32
    )
    total = gathered_total(partial_value, "atom")
    weighted = (green_both[:, None] * total).astype(jnp.bfloat16)
    potential = sent_and_summed(
        jnp.dot(tile, weighted, preferred_element_type=jnp.float32), "wave", 0
    )
    potential_b = potential.astype(jnp.bfloat16)
    pre = jnp.dot(mixed_b, w_feat, preferred_element_type=jnp.float32) + jnp.dot(
        potential_b, w_pot, preferred_element_type=jnp.float32
    )
    activation = jax.nn.silu(pre).astype(jnp.bfloat16)
    return (hidden_in + jnp.dot(activation, w_out, preferred_element_type=jnp.float32)).astype(
        jnp.bfloat16
    )


def solution(mesh):
    placed = (
        P(("atom", "wave"), None),
        P(("atom", "wave")),
        P(None, ("atom", "wave")),
        P(None, "wave"),
        P("wave"),
        P(),
        P(),
        P(),
        P(),
        P(),
    )
    return jax.shard_map(
        shards, mesh=mesh, in_specs=placed, out_specs=P(("atom", "wave"), None), check_vma=False
    )
```

profile of v0, /device:TPU:1, one launch (start us, length us, event | category | flops | bytes accessed | tf_op | source)
XLA Modules:
  0.0 335.3 jit_solution(13022946264362065189)
XLA Ops:
  6.5 0.0 copy-start
  6.5 1.4 broadcast_in_dim.8
  7.9 7.6 %all-to-all-start = ((f32[16,3,512]{2,1,0:T(4,128)}), f32[16,3,512]{2,1,0:T(4,128)S(1)}, u32[]{:S(2)}, u32[]{:S(2)}) async-start(f32[16,3,512]{2,1,0:T(4,128)} %broadcast_in_dim.8), calls=%async_computation | async-start | bytes 262144 | tf_op jit(solution)/shard_map/all_to_all | solution.py:15
  15.5 1.1 fusion.4
  16.6 1.2 fusion.3
  17.8 0.9 convolution_convert_fusion
  18.7 0.7 convert_element_type.35
  19.4 3.0 all-to-all-done
  22.4 1.1 broadcast_in_dim.9
  23.5 3.7 %all-to-all-start.1 = ((bf16[16,512,64]{1,2,0:T(8,128)(2,1)}), bf16[16,512,64]{1,2,0:T(8,128)(2,1)S(1)}, u32[]{:S(2)}, u32[]{:S(2)}) async-start(bf16[16,512,64]{1,2,0:T(8,128)(2,1)} %broadcast_in_dim.9), calls=%async_computation.1 | async-start | bytes 2097152 | tf_op jit(solution)/shard_map/all_to_all | solution.py:15
  27.2 0.0 all-gather.3.cloned.1.call-start
  27.2 157.7 %while.10 = (s32[]{:T(128)}, bf16[8,1024,2048]{2,1,0:T(8,128)(2,1)}, f32[8,3,1024]{2,1,0:T(4,128)S(1)}, f32[3,1024]{1,0:T(4,128)S(1)}, s32[]{:T(128)}, /*index=5*/s32[]{:T(128)}, s32[]{}, s32[]{}) while((s32[]{:T(128)}, bf16[8,1024,2048]{2,1,0:T(8,128)(2,1)}, f32[8,3,1024]{2,1,0:T(4,128)S(1)}, f32[3,1024]{1,0:T(4,128)S(1)}, s32[]{:T(128)}, ...), condition=%wide.region_2.3_spmd, body=%wide.region_1.2_spmd.sunk | while | flops 16777220 | bytes 12657273 | solution.py:57
  27.3 17.3 %fusion.31 = (bf16[1,1024,1024]{2,1,0:T(8,128)(2,1)S(1)}, bf16[1,1024,1024]{2,1,0:T(8,128)(2,1)S(1)}) fusion(f32[1024]{0:T(1024)S(1)} %bitcast.61, f32[1024]{0:T(1024)S(1)} %bitcast.59, f32[1024]{0:T(1024)S(1)} %bitcast.62, f32[1024]{0:T(1024)S(1)} %bitcast.58, f32[1024]{0:T(1024)S(1)} %bitcast.60, f32[1024]{0:T(1024)S(1)} %bitcast.57), kind=kLoop, calls=%fused_computation.4.clone.1 | loop fusion | flops 8388608 | bytes 4218880 | tf_op jit(solution)/shard_map/while/body/eval_jaxpr/concatenate | solution.py:49
  44.5 2.4 maximum_dynamic-update-slice_fusion.2
  47.0 17.3 %fusion.31 = (bf16[1,1024,1024]{2,1,0:T(8,128)(2,1)S(1)}, bf16[1,1024,1024]{2,1,0:T(8,128)(2,1)S(1)}) fusion(f32[1024]{0:T(1024)S(1)} %bitcast.61, f32[1024]{0:T(1024)S(1)} %bitcast.59, f32[1024]{0:T(1024)S(1)} %bitcast.62, f32[1024]{0:T(1024)S(1)} %bitcast.58, f32[1024]{0:T(1024)S(1)} %bitcast.60, f32[1024]{0:T(1024)S(1)} %bitcast.57), kind=kLoop, calls=%fused_computation.4.clone.1 | loop fusion | flops 8388608 | bytes 4218880 | tf_op jit(solution)/shard_map/while/body/eval_jaxpr/concatenate | solution.py:49
  64.2 2.4 maximum_dynamic-update-slice_fusion.2
  66.7 17.3 %fusion.31 = (bf16[1,1024,1024]{2,1,0:T(8,128)(2,1)S(1)}, bf16[1,1024,1024]{2,1,0:T(8,128)(2,1)S(1)}) fusion(f32[1024]{0:T(1024)S(1)} %bitcast.61, f32[1024]{0:T(1024)S(1)} %bitcast.59, f32[1024]{0:T(1024)S(1)} %bitcast.62, f32[1024]{0:T(1024)S(1)} %bitcast.58, f32[1024]{0:T(1024)S(1)} %bitcast.60, f32[1024]{0:T(1024)S(1)} %bitcast.57), kind=kLoop, calls=%fused_computation.4.clone.1 | loop fusion | flops 8388608 | bytes 4218880 | tf_op jit(solution)/shard_map/while/body/eval_jaxpr/concatenate | solution.py:49
  84.0 2.4 maximum_dynamic-update-slice_fusion.2
  86.4 17.3 %fusion.31 = (bf16[1,1024,1024]{2,1,0:T(8,128)(2,1)S(1)}, bf16[1,1024,1024]{2,1,0:T(8,128)(2,1)S(1)}) fusion(f32[1024]{0:T(1024)S(1)} %bitcast.61, f32[1024]{0:T(1024)S(1)} %bitcast.59, f32[1024]{0:T(1024)S(1)} %bitcast.62, f32[1024]{0:T(1024)S(1)} %bitcast.58, f32[1024]{0:T(1024)S(1)} %bitcast.60, f32[1024]{0:T(1024)S(1)} %bitcast.57), kind=kLoop, calls=%fused_computation.4.clone.1 | loop fusion | flops 8388608 | bytes 4218880 | tf_op jit(solution)/shard_map/while/body/eval_jaxpr/concatenate | solution.py:49
  103.7 2.4 maximum_dynamic-update-slice_fusion.2
  106.1 17.3 %fusion.31 = (bf16[1,1024,1024]{2,1,0:T(8,128)(2,1)S(1)}, bf16[1,1024,1024]{2,1,0:T(8,128)(2,1)S(1)}) fusion(f32[1024]{0:T(1024)S(1)} %bitcast.61, f32[1024]{0:T(1024)S(1)} %bitcast.59, f32[1024]{0:T(1024)S(1)} %bitcast.62, f32[1024]{0:T(1024)S(1)} %bitcast.58, f32[1024]{0:T(1024)S(1)} %bitcast.60, f32[1024]{0:T(1024)S(1)} %bitcast.57), kind=kLoop, calls=%fused_computation.4.clone.1 | loop fusion | flops 8388608 | bytes 4218880 | tf_op jit(solution)/shard_map/while/body/eval_jaxpr/concatenate | solution.py:49
  123.4 2.4 maximum_dynamic-update-slice_fusion.2
  125.8 17.3 %fusion.31 = (bf16[1,1024,1024]{2,1,0:T(8,128)(2,1)S(1)}, bf16[1,1024,1024]{2,1,0:T(8,128)(2,1)S(1)}) fusion(f32[1024]{0:T(1024)S(1)} %bitcast.61, f32[1024]{0:T(1024)S(1)} %bitcast.59, f32[1024]{0:T(1024)S(1)} %bitcast.62, f32[1024]{0:T(1024)S(1)} %bitcast.58, f32[1024]{0:T(1024)S(1)} %bitcast.60, f32[1024]{0:T(1024)S(1)} %bitcast.57), kind=kLoop, calls=%fused_computation.4.clone.1 | loop fusion | flops 8388608 | bytes 4218880 | tf_op jit(solution)/shard_map/while/body/eval_jaxpr/concatenate | solution.py:49
  143.1 2.4 maximum_dynamic-update-slice_fusion.2
  145.5 17.3 %fusion.31 = (bf16[1,1024,1024]{2,1,0:T(8,128)(2,1)S(1)}, bf16[1,1024,1024]{2,1,0:T(8,128)(2,1)S(1)}) fusion(f32[1024]{0:T(1024)S(1)} %bitcast.61, f32[1024]{0:T(1024)S(1)} %bitcast.59, f32[1024]{0:T(1024)S(1)} %bitcast.62, f32[1024]{0:T(1024)S(1)} %bitcast.58, f32[1024]{0:T(1024)S(1)} %bitcast.60, f32[1024]{0:T(1024)S(1)} %bitcast.57), kind=kLoop, calls=%fused_computation.4.clone.1 | loop fusion | flops 8388608 | bytes 4218880 | tf_op jit(solution)/shard_map/while/body/eval_jaxpr/concatenate | solution.py:49
  162.8 2.4 maximum_dynamic-update-slice_fusion.2
  165.3 17.3 %fusion.31 = (bf16[1,1024,1024]{2,1,0:T(8,128)(2,1)S(1)}, bf16[1,1024,1024]{2,1,0:T(8,128)(2,1)S(1)}) fusion(f32[1024]{0:T(1024)S(1)} %bitcast.61, f32[1024]{0:T(1024)S(1)} %bitcast.59, f32[1024]{0:T(1024)S(1)} %bitcast.62, f32[1024]{0:T(1024)S(1)} %bitcast.58, f32[1024]{0:T(1024)S(1)} %bitcast.60, f32[1024]{0:T(1024)S(1)} %bitcast.57), kind=kLoop, calls=%fused_computation.4.clone.1 | loop fusion | flops 8388608 | bytes 4218880 | tf_op jit(solution)/shard_map/while/body/eval_jaxpr/concatenate | solution.py:49
  182.6 2.4 maximum_dynamic-update-slice_fusion.2
  184.9 0.0 all-to-all-done.1
  184.9 0.1 copy.14
  185.0 0.0 copy-start.2
  185.0 14.4 %fusion.16 = f32[2048,64]{0,1:T(8,128)} fusion(bf16[8192,64]{0,1:T(8,128)(2,1)S(1)} %bitcast.55, bf16[8192,2048]{1,0:T(8,128)(2,1)} %bitcast.52), kind=kOutput, calls=%fused_computation.33 | convolution fusion | flops 2147483648 | bytes 35127296 | tf_op jit(solution)/shard_map/dot_general | solution.py:75
  199.4 0.0 all-gather.3.cloned.1.call-update
  199.4 0.0 copy-done.2
  199.5 60.8 %all-gather.3.cloned.1.call-done = f32[32768,64]{0,1:T(8,128)} async-done(((f32[2048,64]{0,1:T(8,128)}), f32[32768,64]{0,1:T(8,128)}) %all-gather.3.cloned.1.call-update) | async-done | bytes 8388624 | tf_op jit(solution)/shard_map/all_gather | solution.py:32
  260.3 8.1 %copy.15 = f32[8,8,16,2048]{3,2,1,0:T(8,128)S(1)} copy(f32[8,8,16,2048]{3,1,2,0:T(8,128)} %bitcast.54) | data formatting | bytes 16777216
  268.4 1.7 bitcast_reduce_fusion
  270.1 17.7 %fusion.6 = f32[16,512,64]{1,2,0:T(8,128)} fusion(bf16[16,512,2048]{2,1,0:T(8,128)(2,1)} %bitcast.53, f32[2048,64]{0,1:T(8,128)S(1)} %bitcast_reduce_fusion, f32[2048]{0:T(1024)S(1)} %pad_maximum_fusion), kind=kOutput, calls=%fused_computation.22 | convolution fusion | flops 2147745792 | bytes 36184064 | tf_op jit(solution)/shard_map/dot_general | solution.py:81
  287.8 0.0 copy-start.3
  287.8 6.7 %all-to-all-start.2 = ((f32[16,512,64]{1,2,0:T(8,128)}), f32[16,512,64]{1,2,0:T(8,128)S(1)}, u32[]{:S(2)}, u32[]{:S(2)}) async-start(f32[16,512,64]{1,2,0:T(8,128)} %fusion.6), calls=%async_computation.2 | async-start | bytes 4194304 | tf_op jit(solution)/shard_map/all_to_all | solution.py:42
  294.5 0.0 copy-done
  294.5 0.2 fusion.15
  294.7 32.4 %all-to-all-done.2 = f32[16,512,64]{1,2,0:T(8,128)S(1)} async-done(((f32[16,512,64]{1,2,0:T(8,128)}), f32[16,512,64]{1,2,0:T(8,128)S(1)}, u32[]{:S(2)}, u32[]{:S(2)}) %all-to-all-start.2) | async-done | bytes 2097184 | tf_op jit(solution)/shard_map/all_to_all | solution.py:42
  327.1 0.2 reduce_sum.29
  327.3 0.0 copy-done.1
  327.3 0.0 copy-done.3
  327.3 0.0 copy-done.4
  327.3 1.1 fusion.2
  (21 shorter events, 0.2 us)
Async XLA Ops:
  6.5 288.0 %copy-start = (bf16[128,256]{1,0:T(8,128)(2,1)S(1)}, bf16[128,256]{1,0:T(8,128)(2,1)}, u32[]{:S(2)}) copy-start(bf16[128,256]{1,0:T(8,128)(2,1)} %param.19) | copy-start | bytes 196612
  7.9 14.4 %all-to-all-start = ((f32[16,3,512]{2,1,0:T(4,128)}), f32[16,3,512]{2,1,0:T(4,128)S(1)}, u32[]{:S(2)}, u32[]{:S(2)}) async-start(f32[16,3,512]{2,1,0:T(4,128)} %broadcast_in_dim.8), calls=%async_computation | async-start | bytes 262144 | tf_op jit(solution)/shard_map/all_to_all | solution.py:15
  23.5 161.4 %all-to-all-start.1 = ((bf16[16,512,64]{1,2,0:T(8,128)(2,1)}), bf16[16,512,64]{1,2,0:T(8,128)(2,1)S(1)}, u32[]{:S(2)}, u32[]{:S(2)}) async-start(bf16[16,512,64]{1,2,0:T(8,128)(2,1)} %broadcast_in_dim.9), calls=%async_computation.1 | async-start | bytes 2097152 | tf_op jit(solution)/shard_map/all_to_all | solution.py:15
  27.2 233.1 %all-gather.3.cloned.1.call-start = ((), (), s32[]{:S(2)}) async-start(), calls=%async_computation.3 | async-start | bytes 8912896 | tf_op jit(solution)/shard_map/all_gather | solution.py:32
  185.0 14.4 %copy-start.2 = (f32[1024]{0:T(1024)S(1)}, f32[1024]{0:T(1024)}, u32[]{:S(2)}) copy-start(f32[1024]{0:T(1024)} %param.16) | copy-start | bytes 12292
  287.8 39.5 %copy-start.1 = (bf16[512,128]{1,0:T(8,128)(2,1)S(1)}, bf16[512,128]{1,0:T(8,128)(2,1)}, u32[]{:S(2)}) copy-start(bf16[512,128]{1,0:T(8,128)(2,1)} %param.12) | copy-start | bytes 393220
  287.8 39.5 %copy-start.3 = (bf16[256,128]{1,0:T(8,128)(2,1)S(1)}, bf16[256,128]{1,0:T(8,128)(2,1)}, u32[]{:S(2)}) copy-start(bf16[256,128]{1,0:T(8,128)(2,1)} %param.21) | copy-start | bytes 196612
  287.8 39.5 %copy-start.4 = (bf16[64,256]{1,0:T(8,128)(2,1)S(1)}, bf16[64,256]{1,0:T(8,128)(2,1)}, u32[]{:S(2)}) copy-start(bf16[64,256]{1,0:T(8,128)(2,1)} %param.20) | copy-start | bytes 98308
  287.8 39.3 %all-to-all-start.2 = ((f32[16,512,64]{1,2,0:T(8,128)}), f32[16,512,64]{1,2,0:T(8,128)S(1)}, u32[]{:S(2)}, u32[]{:S(2)}) async-start(f32[16,512,64]{1,2,0:T(8,128)} %fusion.6), calls=%async_computation.2 | async-start | bytes 4194304 | tf_op jit(solution)/shard_map/all_to_all | solution.py:42
Sparse Core Ops, SparseCore 0:
  199.6 60.6 all-gather.2
where the time goes:
time: 336 us; the launch traced here: 335 us
  other arithmetic  161 us (48%)
  waiting for transfers between devices  96.2 us (29%)
  matrix products  35.5 us (11%)
  starting transfers between devices  18 us (5%)
  between operations  13.5 us (4%)
  local copies, waits for them, and re-layouts  10.9 us (3%)
    concatenate x8, other arithmetic, phases(): jnp.concatenate([jnp.cos(angle), jnp.sin(angle)], axis=1)  138 us
    all_gather x1, waiting for transfers between devices, gathered_total(): return lax.all_gather(array, axis).sum(0)  60.8 us
    all_to_all x1, waiting for transfers between devices, sent_and_summed(): lax.all_to_all(parts, axis, split_axis=0, concat_axis=0, tiled=True)  32.4 us
    dynamic_update_slice x8, other arithmetic, phase_tile(): tiles = lax.map(lambda block: phases(block, waves), blocks)  19.2 us
    dot_general x1, matrix products, shards(): jnp.dot(tile, weighted, preferred_element_type=jnp.float32)  17.7 us
    dot_general x1, matrix products, shards(): lax.dot_general(tile, block_charges, (((0,), (0,)), ((), ())), preferred_...  14.4 us
    all_to_all x2, starting transfers between devices, copy_for_each(): lax.all_to_all(jnp.broadcast_to(array[None], (devices, *array.shape)), ax...  11.3 us
    unnamed x11, local copies, waits for them, and re-layouts  8.13 us
  transfers between devices with their start and end apart: 4, of which 3 were waited for; matrix products, arithmetic and copies ran while one was open for 48% of the time, Pallas kernels for 0%

commit v1 on v0

v1 whole, which is shorter than its diff:
```python
import functools

import jax
import jax.numpy as jnp
from jax import lax
from jax.experimental import pallas as pl
from jax.experimental.pallas import tpu as pltpu
from jax.sharding import PartitionSpec as P

EPS = 1e-06
N = 16
ATOMS = 512
Q = 64
MAIN = 64 * N
ROWS = MAIN + 9 * N
SHARD = 80
COS = (0.9999999890590228, -19.739204499453827, 64.9391174598908, -85.45013953079768, 60.16763095026347, -25.967599245923736, 6.52865815775625)
SIN = (6.2831853025115025, -41.341700405317205, 81.60513138578321, -76.70301535364746, 42.02592698447418, -14.8998466635365, 3.2381375046186873)
F32 = jnp.float32
BF16 = jnp.bfloat16
NT = (((1,), (1,)), ((), ()))
TN = (((0,), (0,)), ((), ()))


def dot(a, b, dims=(((1,), (0,)), ((), ()))):
    return lax.dot_general(a, b, dims, preferred_element_type=F32)


def poly(u, coeffs):
    total = jnp.full_like(u, coeffs[-1])
    for c in coeffs[-2::-1]:
        total = total * u + c
    return total


def waves_of(x):
    j = lax.broadcasted_iota(jnp.int32, (N, x.shape[1]), 0).astype(F32) + 1.0
    turns = j * x
    r = turns - jnp.round(turns)
    u = r * r
    return poly(u, COS), r * poly(u, SIN)


def green_rows(n1, n2, n3, g, atom, key=None):
    count = n1.shape[1]
    first = jnp.where(n1 != 0, n1, jnp.where(n2 != 0, n2, n3))
    s = jnp.where(first < 0, -1, 1)
    a1, a2, a3 = jnp.abs(n1), jnp.abs(n2), jnp.abs(n3)
    s2 = jnp.where(n2 * s < 0, -1.0, 1.0)
    s3 = jnp.where(n3 * s < 0, -1.0, 1.0)
    row = lax.broadcasted_iota(jnp.int32, (8 * N, count), 0)
    owner, kind = lax.div(row, 8) + 1, lax.rem(row, 8)
    factor = jnp.where((kind == 1) | (kind == 5), s2, 1.0)
    factor = jnp.where(kind == 2, s3, factor)
    factor = jnp.where(kind == 3, s2 * s3, factor)
    inside = a3 == owner
    flat = (a3 == 0) & (a1 == owner)
    line = (a3 == 0) & (n1 == 0) & (a2 == owner)
    hit = jnp.where(kind < 4, inside.astype(F32), jnp.where(kind < 6, flat.astype(F32), line.astype(F32)))
    hit = jnp.where(kind == 7, 0.0, hit)
    left = hit * factor * g
    lane = lax.broadcasted_iota(jnp.int32, (32, count), 0)
    mine = atom + 1
    one, zero = jnp.ones((1, count), F32), jnp.zeros((1, count), F32)
    is1, is2 = (a1 == mine).astype(F32), (a2 == mine).astype(F32)
    no1, no2 = (n1 == 0).astype(F32), (n2 == 0).astype(F32)
    right = jnp.where(lane < N, is1 * (a2 == lane + 1).astype(F32), zero)
    right = jnp.where((lane >= 16) & (lane < 18), is1 * no2, right)
    right = jnp.where((lane >= 18) & (lane < 20), no1 * is2, right)
    right = jnp.where((lane >= 20) & (lane < 24), is2, right)
    right = jnp.where(lane == 24, no1 * no2, right)
    right = jnp.where((lane >= 25) & (lane < 27), no2, right)
    right = jnp.where((lane >= 27) & (lane < 29), one, right)
    right = jnp.concatenate([right, jnp.zeros((96, count), F32)]).astype(BF16)
    total = None
    for _ in range(3):
        piece = left.astype(BF16)
        left = left - piece.astype(F32)
        part = dot(piece, right, NT)
        total = part if total is None else total + part
    return total


def apply_green(t, gt):
    lanes = lax.broadcasted_iota(jnp.int32, (N, 128), 1)
    sign = jnp.where(lanes < Q, -1.0, 1.0)

    def swap(v):
        return jnp.concatenate([v[:, Q:], v[:, :Q]], axis=1)

    cc, cs, sc, ss = t[0:16], t[16:32], t[32:48], t[48:64]
    g0, g2, g3, g23 = (gt[0:16, k : k + 1] for k in range(4))
    xcc, xcs, xsc, xss = sign * swap(cc), sign * swap(cs), sign * swap(sc), sign * swap(ss)
    out = [
        g0 * cc - g2 * ss + g3 * xsc + g23 * xcs,
        g0 * cs + g2 * sc - g23 * xcc + g3 * xss,
        g0 * sc + g2 * cs - g3 * xcc + g23 * xss,
        g0 * ss - g2 * cc - g23 * xsc - g3 * xcs,
    ]
    e = t[64:80]
    r = lax.broadcasted_iota(jnp.int32, (N, 128), 0)
    h = [jnp.broadcast_to(gt[16:32, k : k + 1], (N, 128)) for k in range(8)]
    even = lax.rem(r, 2) == 0
    e0 = jnp.where(r < 4, h[0], jnp.where(r < 8, h[4], jnp.where(r == 8, h[0], jnp.where(r < 11, h[4], h[6]))))
    e0 = jnp.where(r < 13, e0, 0.0)
    e3 = jnp.where(r < 4, jnp.where(even, h[2], -h[2]), 0.0)
    e2 = jnp.where((r >= 4) & (r < 8), jnp.where(r < 6, -h[5], h[5]), 0.0)
    up = jnp.concatenate([e[1:], e[:1]], axis=0)
    down = jnp.concatenate([e[-1:], e[:-1]], axis=0)
    pair = jnp.where(even, up, down)
    out.append(e0 * e + e3 * (sign * swap(pair)) + e2 * pair)
    return jnp.concatenate(out, axis=0)


def kernel(
    feat, species, coords, widx, green, embed, w_charge, w_feat, w_pot, w_out, out,
    cbuf, xbuf, gbuf, gsend, ebuf, zbuf, tabs, tmain, tedge, tsend, trecv, wall, wmain, wedge, wt,
    psend, precv, mixed, pre,
    cs_sem, cr_sem, xs_sem, xr_sem, gs_sem, gr_sem, ts_sem, tr_sem, ws_sem, wr_sem, ps_sem, pr_sem,
):
    atom, wave = lax.axis_index("atom"), lax.axis_index("wave")

    def wave_peer(d):
        y = lax.rem(lax.div(wave, 4) + lax.div(d, 4), 4)
        x = lax.rem(lax.rem(wave, 4) + lax.rem(d, 4), 4)
        return y * 4 + x

    def wave_source(d):
        y = lax.rem(lax.div(wave, 4) + 4 - lax.div(d, 4), 4)
        x = lax.rem(lax.rem(wave, 4) + 4 - lax.rem(d, 4), 4)
        return y * 4 + x

    def atom_peer(d):
        z = lax.rem(lax.div(atom, 2) + lax.div(d, 2), 8)
        return z * 2 + lax.rem(lax.rem(atom, 2) + lax.rem(d, 2), 2)

    def atom_source(d):
        z = lax.rem(lax.div(atom, 2) + 8 - lax.div(d, 2), 8)
        return z * 2 + lax.rem(lax.rem(atom, 2) + lax.rem(d, 2), 2)

    def push(src, dst, ssem, rsem, axis, peer):
        return pltpu.make_async_remote_copy(
            src_ref=src, dst_ref=dst, send_sem=ssem, recv_sem=rsem,
            device_id={axis: peer}, device_id_type=pl.DeviceIdType.MESH,
        )

    def each(body):
        def step(d, carry):
            body(d)
            return carry

        lax.fori_loop(1, N, step, 0)

    barrier = pltpu.get_barrier_semaphore()

    @each
    def _(d):
        pl.semaphore_signal(barrier, inc=1, device_id={"wave": wave_peer(d)}, device_id_type=pl.DeviceIdType.MESH)
        pl.semaphore_signal(barrier, inc=1, device_id={"atom": atom_peer(d)}, device_id_type=pl.DeviceIdType.MESH)

    hidden = feat[...].astype(F32)
    scale = lax.rsqrt(jnp.mean(hidden * hidden, axis=1, keepdims=True) + EPS)
    kinds = lax.broadcasted_iota(jnp.int32, (16, ATOMS), 0)
    onehot = (kinds == species[...]).astype(F32).astype(BF16)
    mixed_b = (hidden * scale + dot(onehot, embed[...], TN)).astype(BF16)
    mixed[...] = mixed_b
    charges = dot(mixed_b, w_charge[...])
    cbuf[wave] = charges.T.astype(BF16)
    xbuf[wave] = coords[...]

    pl.semaphore_wait(barrier, 2 * (N - 1))

    def c_copy(d, slot):
        return push(cbuf.at[slot], cbuf.at[slot], cs_sem.at[d], cr_sem.at[slot], "wave", wave_peer(d))

    def x_copy(d, slot):
        return push(xbuf.at[slot], xbuf.at[slot], xs_sem.at[d], xr_sem.at[slot], "wave", wave_peer(d))

    @each
    def _(d):
        x_copy(d, wave).start()
        c_copy(d, wave).start()

    grid = green_rows(widx[0:1], widx[1:2], widx[2:3], green[...], atom)
    for k in range(N):
        gsend[k] = grid[8 * k : 8 * k + 8]
    gbuf[wave] = gsend[wave]

    def g_copy(d, slot):
        return push(gsend.at[wave_peer(d)], gbuf.at[slot], gs_sem.at[d], gr_sem.at[slot], "wave", wave_peer(d))

    @each
    def _(d):
        g_copy(d, wave).start()

    tmain[...] = jnp.zeros_like(tmain)
    tedge[...] = jnp.zeros_like(tedge)

    def add_block(slot):
        place = xbuf[slot]
        xc, xs = waves_of(place[0:1])
        yc, ys = waves_of(place[1:2])
        zc, zs = waves_of(place[2:3])
        for k, table in enumerate((xc, xs, yc, ys, zc, zs)):
            tabs[k] = table
        xcw, xsw, ycw, ysw, zcw, zsw = (tabs[k, pl.ds(wave, 1), :] for k in range(6))
        for i in range(N):
            a, b = xc[i : i + 1], xs[i : i + 1]
            block = jnp.concatenate([a * yc, a * ys, b * yc, b * ys], axis=0)
            ebuf[slot, 64 * i : 64 * i + 64, :] = block.astype(BF16)
        r = lax.broadcasted_iota(jnp.int32, (N, ATOMS), 0)
        rest = jnp.where(r == 0, 1.0, 0.0)
        for k, row in enumerate((xcw, xsw, ycw, ysw)):
            rest = jnp.where(r == k + 1, row, rest)
        edge = (xc, xs, yc, ys, xcw * yc, xsw * ys, xsw * yc, xcw * ys, rest)
        for k, part in enumerate(edge):
            ebuf[slot, MAIN + N * k : MAIN + N * (k + 1), :] = part.astype(BF16)
        zbuf[slot] = jnp.concatenate([zcw, zsw, jnp.zeros((6, ATOMS), F32)], axis=0)
        c = cbuf[slot]
        wide = c.astype(F32)
        cz = jnp.concatenate([zcw * wide, zsw * wide], axis=0).astype(BF16)
        full = jnp.concatenate([cz, c, jnp.zeros((Q, ATOMS), BF16)], axis=0)
        for k in range(4):
            rows = slice(256 * k, 256 * k + 256)
            tmain[rows, :] += dot(ebuf[slot, rows, :], cz, NT)
        tedge[...] += dot(ebuf[slot, MAIN:, :], full, NT)

    add_block(wave)

    @each
    def _(d):
        slot = wave_source(d)
        x_copy(d, slot).wait_recv()
        c_copy(d, slot).wait_recv()
        add_block(slot)

    r = lax.broadcasted_iota(jnp.int32, (9 * N, 128), 0)
    flat = ((r >= 4 * N) & (r < 8 * N)) | (r > 8 * N)
    wedge[...] = jnp.where(flat, tedge[:, 128:], tedge[:, :128])
    for i in range(N):
        tsend[i, 0:64, :] = tmain[64 * i : 64 * i + 64, :].astype(BF16)
        tail = jnp.concatenate([wedge[pl.ds(i, 8, stride=N), :], wedge[8 * N : 8 * N + 8, :]], axis=0)
        tsend[i, 64:80, :] = tail.astype(BF16)

    def t_copy(d, slot):
        return push(tsend.at[atom_peer(d)], trecv.at[slot], ts_sem.at[d], tr_sem.at[slot], "atom", atom_peer(d))

    @each
    def _(d):
        t_copy(d, atom).start()

    trecv[atom] = tsend[atom]
    pre[...] = dot(mixed[...], w_feat[...])

    @each
    def _(d):
        g_copy(d, wave_source(d)).wait_recv()

    gsum = gbuf[0]
    for k in range(1, N):
        gsum = gsum + gbuf[k]
    columns = jnp.concatenate([gsum, jnp.zeros((120, 128), F32)], axis=0).T

    @each
    def _(d):
        t_copy(d, atom_source(d)).wait_recv()

    total = trecv[0].astype(F32)
    for k in range(1, N):
        total = total + trecv[k].astype(F32)
    wall[atom] = apply_green(total, columns).astype(BF16)

    def w_copy(d, slot):
        return push(wall.at[slot], wall.at[slot], ws_sem.at[d], wr_sem.at[slot], "atom", atom_peer(d))

    @each
    def _(d):
        w_copy(d, atom).start()

    @each
    def _(d):
        w_copy(d, atom_source(d)).wait_recv()

    for i in range(N):
        shard = wall[i].astype(F32)
        wmain[64 * i : 64 * i + 64, :] = shard[0:64]
        wedge[pl.ds(i, 8, stride=N), :] = shard[64:72]
        if i == 0:
            wedge[8 * N : 9 * N, :] = jnp.concatenate([shard[72:80], jnp.zeros((8, 128), F32)], axis=0)
    for k in range(8):
        wt[0:128, 128 * k : 128 * k + 128] = wmain[128 * k : 128 * k + 128, :].T.astype(BF16)
    wt[128:192, 0:MAIN] = jnp.zeros((64, MAIN), BF16)
    edges = wedge[...]
    low = jnp.where(flat, 0.0, edges)
    high = jnp.where(flat, edges, 0.0)
    blank = jnp.zeros((112, 128), F32)
    low_t = jnp.concatenate([low[:128].T, jnp.concatenate([low[128:], blank], axis=0).T], axis=1)
    high_t = jnp.concatenate([high[:128].T, jnp.concatenate([high[128:], blank], axis=0).T], axis=1)
    wt[0:128, MAIN:] = low_t[:, : 9 * N].astype(BF16)
    wt[128:192, MAIN:] = high_t[:Q, : 9 * N].astype(BF16)

    def p_copy(d, slot):
        return push(psend.at[wave_peer(d)], precv.at[slot], ps_sem.at[d], pr_sem.at[slot], "wave", wave_peer(d))

    def partial(slot):
        u = dot(wt[...], ebuf[slot])
        z = zbuf[slot]
        return (z[0:1] * u[0:Q] + z[1:2] * u[Q : 2 * Q] + u[2 * Q :]).astype(BF16)

    @each
    def _(d):
        slot = wave_peer(d)
        psend[slot] = partial(slot)
        p_copy(d, wave).start()

    precv[wave] = partial(wave)

    @each
    def _(d):
        p_copy(d, wave_source(d)).wait_recv()

    potential = precv[0].astype(F32)
    for k in range(1, N):
        potential = potential + precv[k].astype(F32)
    potential_b = potential.T.astype(BF16)
    before = pre[...] + dot(potential_b, w_pot[...])
    activation = (before / (1.0 + jnp.exp(-before))).astype(BF16)
    out[...] = (feat[...].astype(F32) + dot(activation, w_out[...])).astype(BF16)

    @each
    def _(d):
        x_copy(d, wave).wait_send()
        c_copy(d, wave).wait_send()
        g_copy(d, wave).wait_send()
        t_copy(d, atom).wait_send()
        w_copy(d, atom).wait_send()
        p_copy(d, wave).wait_send()


def shards(features, species, coords, wave_index, green, embed, w_charge, w_feat, w_pot, w_out):
    vmem = pl.BlockSpec(memory_space=pltpu.VMEM)
    dma = pltpu.SemaphoreType.DMA((N,))
    return pl.pallas_call(
        kernel,
        out_shape=jax.ShapeDtypeStruct(features.shape, BF16),
        in_specs=[vmem] * 10,
        out_specs=vmem,
        scratch_shapes=[
            pltpu.VMEM((N, Q, ATOMS), BF16),
            pltpu.VMEM((N, 3, ATOMS), F32),
            pltpu.VMEM((N, 8, 128), F32),
            pltpu.VMEM((N, 8, 128), F32),
            pltpu.VMEM((N, ROWS, ATOMS), BF16),
            pltpu.VMEM((N, 8, ATOMS), F32),
            pltpu.VMEM((6, N, ATOMS), F32),
            pltpu.VMEM((MAIN, 128), F32),
            pltpu.VMEM((9 * N, 256), F32),
            pltpu.VMEM((N, SHARD, 128), BF16),
            pltpu.VMEM((N, SHARD, 128), BF16),
            pltpu.VMEM((N, SHARD, 128), BF16),
            pltpu.VMEM((MAIN, 128), F32),
            pltpu.VMEM((9 * N, 128), F32),
            pltpu.VMEM((192, ROWS), BF16),
            pltpu.VMEM((N, Q, ATOMS), BF16),
            pltpu.VMEM((N, Q, ATOMS), BF16),
            pltpu.VMEM((ATOMS, 128), BF16),
            pltpu.VMEM((ATOMS, 256), F32),
        ]
        + [dma] * 12,
        compiler_params=pltpu.CompilerParams(
            collective_id=0, has_side_effects=True, vmem_limit_bytes=60 * 1024 * 1024
        ),
        name="ewald",
    )(
        features, species.reshape(1, -1), coords, wave_index, green.reshape(1, -1),
        embed, w_charge, w_feat, w_pot, w_out,
    )


def solution(mesh):
    placed = (
        P(("atom", "wave"), None),
        P(("atom", "wave")),
        P(None, ("atom", "wave")),
        P(None, "wave"),
        P("wave"),
        P(),
        P(),
        P(),
        P(),
        P(),
    )
    return jax.shard_map(
        shards, mesh=mesh, in_specs=placed, out_specs=P(("atom", "wave"), None), check_vma=False
    )
```

time: 336 us -> 74.3 us (0.22)
  other arithmetic: 161 us -> 0 us
  waiting for transfers between devices: 96.2 us -> 0 us
  Pallas kernels: 0 us -> 71.1 us
  matrix products: 35.5 us -> 0 us
  starting transfers between devices: 18 us -> 0 us
  between operations: 13.5 us -> 0.01 us
  local copies, waits for them, and re-layouts: 10.9 us -> 3 us
    concatenate x9 -> x0, other arithmetic: 138 us -> none  [the longest x8 138 us: phases(): jnp.concatenate([jnp.cos(angle), jnp.sin(angle)], axis=1)]
    pallas_call x0 -> x1, Pallas kernels: none -> 71.1 us  [shards(): pl.pallas_call(kernel, out_shape=jax.ShapeDtypeStruct(features.shape, BF1...]
    all_gather x1 -> x0, waiting for transfers between devices: 60.8 us -> none  [gathered_total(): return lax.all_gather(array, axis).sum(0)]
    dot_general x6 -> x0, matrix products: 35.5 us -> none  [the longest x1 17.7 us: shards(): jnp.dot(tile, weighted, preferred_element_type=jnp.float32)]
    all_to_all x3 -> x0, waiting for transfers between devices: 35.4 us -> none  [the longest x1 32.4 us: sent_and_summed(): lax.all_to_all(parts, axis, split_axis=0, concat_axis=0, tiled=True)]
    dynamic_update_slice x8 -> x0, other arithmetic: 19.2 us -> none  [phase_tile(): tiles = lax.map(lambda block: phases(block, waves), blocks)]
    all_to_all x3 -> x0, starting transfers between devices: 17.9 us -> none  [the longest x2 11.3 us: copy_for_each(): lax.all_to_all(jnp.broadcast_to(array[None], (devices, *array.shape)), ax...]
    unnamed x11 -> x2, local copies, waits for them, and re-layouts: 8.13 us -> 3 us
  transfers between devices with their start and end apart: 4 -> 0, of which waited for: 3 -> 0; matrix products, arithmetic and copies ran while one was open for 48% -> 0% of each run, Pallas kernels for 0% -> 0%
where the time goes in v1:
time: 74.3 us; the launch traced here: 74.2 us
  Pallas kernels  71.1 us (96%)
  local copies, waits for them, and re-layouts  3 us (4%)
    pallas_call x1, Pallas kernels, shards(): pl.pallas_call(kernel, out_shape=jax.ShapeDtypeStruct(features.shape, BF1...  71.1 us
    unnamed x2, local copies, waits for them, and re-layouts  3 us

profile of v1, /device:TPU:1, one launch (start us, length us, event | category | flops | bytes accessed | tf_op | source)
XLA Modules:
  0.0 74.2 jit_solution(17620780661338859048)
XLA Ops:
  0.0 1.4 %copy.11.w_charge = bf16[128,64]{1,0:T(8,128)(2,1)} copy(bf16[128,64]{0,1:T(8,128)(2,1)} %param.16) | data formatting | bytes 32768 | tf_op args[6]
  1.4 71.1 %ewald.1 = bf16[512,128]{1,0:T(8,128)(2,1)} custom-call(bf16[512,128]{1,0:T(8,128)(2,1)} %feat.1, s32[1,512]{1,0:T(1,128)} %bitcast.3, f32[3,512]{1,0:T(4,128)} %coords.1, s32[3,1024]{1,0:T(4,128)} %widx.1, f32[1,1024]{1,0:T(1,128)} %bitcast.2, bf16[16,128]{1,0:T(8,128)(2,1)} %embed.1, bf16[128,64]{1,0:T(8,128)(2,1)} %copy.11.w_charge, ...), custom_call_target="tpu_custom_call" | custom-call | tf_op jit(solution)/shard_map/ewald/pallas_call | solution.py:343
  72.6 1.6 %copy.13 = bf16[512,128]{1,0:T(8,128)(2,1)} copy(bf16[512,128]{1,0:T(8,128)(2,1)} %ewald.1) | data formatting | bytes 262144

commit v2 on v1

v2 whole, which is shorter than its diff:
```python
import functools

import jax
import jax.numpy as jnp
from jax import lax
from jax.experimental import pallas as pl
from jax.experimental.pallas import tpu as pltpu
from jax.sharding import PartitionSpec as P

EPS = 1e-06
N = 16
ATOMS = 512
Q = 64
MAIN = 64 * N
LOW = MAIN + 5 * N
ROWS = LOW + 5 * N
SHARD = 80
COS = (0.9999999890590228, -19.739204499453827, 64.9391174598908, -85.45013953079768, 60.16763095026347, -25.967599245923736, 6.52865815775625)
SIN = (6.2831853025115025, -41.341700405317205, 81.60513138578321, -76.70301535364746, 42.02592698447418, -14.8998466635365, 3.2381375046186873)
F32 = jnp.float32
BF16 = jnp.bfloat16
NT = (((1,), (1,)), ((), ()))
TN = (((0,), (0,)), ((), ()))


def dot(a, b, dims=(((1,), (0,)), ((), ()))):
    return lax.dot_general(a, b, dims, preferred_element_type=F32)


def poly(u, coeffs):
    total = jnp.full_like(u, coeffs[-1])
    for c in coeffs[-2::-1]:
        total = total * u + c
    return total


def waves_of(x):
    j = lax.broadcasted_iota(jnp.int32, (8, x.shape[1]), 0).astype(F32) + 1.0
    turns = j * x
    r = turns - jnp.round(turns)
    u = r * r
    c, s = poly(u, COS), r * poly(u, SIN)
    c8, s8 = c[7:8], s[7:8]
    return jnp.concatenate([c, c8 * c - s8 * s], axis=0), jnp.concatenate([s, s8 * c + c8 * s], axis=0)


def green_rows(n1, n2, n3, g, atom, key=None):
    count = n1.shape[1]
    first = jnp.where(n1 != 0, n1, jnp.where(n2 != 0, n2, n3))
    s = jnp.where(first < 0, -1, 1)
    a1, a2, a3 = jnp.abs(n1), jnp.abs(n2), jnp.abs(n3)
    s2 = jnp.where(n2 * s < 0, -1.0, 1.0)
    s3 = jnp.where(n3 * s < 0, -1.0, 1.0)
    row = lax.broadcasted_iota(jnp.int32, (8 * N, count), 0)
    owner, kind = lax.div(row, 8) + 1, lax.rem(row, 8)
    factor = jnp.where((kind == 1) | (kind == 5), s2, 1.0)
    factor = jnp.where(kind == 2, s3, factor)
    factor = jnp.where(kind == 3, s2 * s3, factor)
    inside = a3 == owner
    flat = (a3 == 0) & (a1 == owner)
    line = (a3 == 0) & (n1 == 0) & (a2 == owner)
    hit = jnp.where(kind < 4, inside.astype(F32), jnp.where(kind < 6, flat.astype(F32), line.astype(F32)))
    hit = jnp.where(kind == 7, 0.0, hit)
    left = hit * factor * g
    lane = lax.broadcasted_iota(jnp.int32, (32, count), 0)
    mine = atom + 1
    one, zero = jnp.ones((1, count), F32), jnp.zeros((1, count), F32)
    is1, is2 = (a1 == mine).astype(F32), (a2 == mine).astype(F32)
    no1, no2 = (n1 == 0).astype(F32), (n2 == 0).astype(F32)
    right = jnp.where(lane < N, is1 * (a2 == lane + 1).astype(F32), zero)
    right = jnp.where((lane >= 16) & (lane < 18), is1 * no2, right)
    right = jnp.where((lane >= 18) & (lane < 20), no1 * is2, right)
    right = jnp.where((lane >= 20) & (lane < 24), is2, right)
    right = jnp.where(lane == 24, no1 * no2, right)
    right = jnp.where((lane >= 25) & (lane < 27), no2, right)
    right = jnp.where((lane >= 27) & (lane < 29), one, right)
    right = jnp.concatenate([right, jnp.zeros((96, count), F32)]).astype(BF16)
    total = None
    for _ in range(3):
        piece = left.astype(BF16)
        left = left - piece.astype(F32)
        part = dot(piece, right, NT)
        total = part if total is None else total + part
    return total


def apply_green(t, gt):
    lanes = lax.broadcasted_iota(jnp.int32, (N, 128), 1)
    sign = jnp.where(lanes < Q, -1.0, 1.0)

    def swap(v):
        return jnp.concatenate([v[:, Q:], v[:, :Q]], axis=1)

    cc, cs, sc, ss = t[0:16], t[16:32], t[32:48], t[48:64]
    g0, g2, g3, g23 = (gt[0:16, k : k + 1] for k in range(4))
    xcc, xcs, xsc, xss = sign * swap(cc), sign * swap(cs), sign * swap(sc), sign * swap(ss)
    out = [
        g0 * cc - g2 * ss + g3 * xsc + g23 * xcs,
        g0 * cs + g2 * sc - g23 * xcc + g3 * xss,
        g0 * sc + g2 * cs - g3 * xcc + g23 * xss,
        g0 * ss - g2 * cc - g23 * xsc - g3 * xcs,
    ]
    e = t[64:80]
    r = lax.broadcasted_iota(jnp.int32, (N, 128), 0)
    h = [jnp.broadcast_to(gt[16:32, k : k + 1], (N, 128)) for k in range(8)]
    even = lax.rem(r, 2) == 0
    e0 = jnp.where(r < 4, h[0], jnp.where(r < 8, h[4], jnp.where(r == 8, h[0], jnp.where(r < 11, h[4], h[6]))))
    e0 = jnp.where(r < 13, e0, 0.0)
    e3 = jnp.where(r < 4, jnp.where(even, h[2], -h[2]), 0.0)
    e2 = jnp.where((r >= 4) & (r < 8), jnp.where(r < 6, -h[5], h[5]), 0.0)
    up = jnp.concatenate([e[1:], e[:1]], axis=0)
    down = jnp.concatenate([e[-1:], e[:-1]], axis=0)
    pair = jnp.where(even, up, down)
    out.append(e0 * e + e3 * (sign * swap(pair)) + e2 * pair)
    return jnp.concatenate(out, axis=0)


def pick(k, values):
    out = values[-1]
    for j in range(len(values) - 2, -1, -1):
        out = jnp.where(k == j, values[j], out)
    return out


def kernel(
    feat_in, species_in, coords_in, widx_in, green_in, embed_in, wc_in, wf_in, wp_in, wo_in, out,
    feat, species, coords, widx, green, embed, w_charge_t, w_feat, w_pot, w_out,
    cbuf, xbuf, gbuf, gsend, ebuf, zbuf, tabs, tabs_too, czs, tmain, tedge, wedge, thalf, tother, tsend, trecv, wall, wt,
    psend, precv, prelay, mixed, pre,
    in_sem, send_sem, cr_sem, xr_sem, gr_sem, th_sem, tr_sem, wr_sem, pr_sem, pq_sem,
):
    atom, wave = lax.axis_index("atom"), lax.axis_index("wave")
    here_y, here_x = lax.div(wave, 4), lax.rem(wave, 4)
    z, core = lax.div(atom, 2), lax.rem(atom, 2)
    partner = 2 * z + 1 - core
    ahead = 1 + 2 * core
    back = 3 - 2 * core

    def at(dy, dx):
        return lax.rem(here_y + dy, 4) * 4 + lax.rem(here_x + dx, 4)

    def opposite(dy, dx):
        return at(4 - dy, 4 - dx)

    PLACE_Y = (3, 1, 1, 3, 0, ahead, 0, back, 2, 1, 2, 3, 0, 2, 2)
    PLACE_X = (1, 1, 3, 3, ahead, 0, back, 0, 1, 2, 3, 2, 2, 0, 2)
    STEP_Y = (3, 0, 1, 0, 0, ahead, ahead)
    STEP_X = (0, 1, 0, 3, ahead, 0, ahead)
    corner = 1 + 2 * core

    def z_atom(dz, side):
        return 2 * lax.rem(z + dz, 8) + side

    def push(src, dst, ssem, rsem, axis, peer):
        return pltpu.make_async_remote_copy(
            src_ref=src, dst_ref=dst, send_sem=ssem, recv_sem=rsem,
            device_id={axis: peer}, device_id_type=pl.DeviceIdType.MESH,
        )

    def times(count, body, start=0):
        def step(k, carry):
            body(k)
            return carry

        lax.fori_loop(start, count, step, 0)

    barrier = pltpu.get_barrier_semaphore()

    def greet(axis, peer):
        pl.semaphore_signal(barrier, inc=1, device_id={axis: peer}, device_id_type=pl.DeviceIdType.MESH)

    for d in (4, 3, 5, 2, 6, 1, 7):
        greet("atom", z_atom(d, core))
    times(N, lambda d: greet("wave", at(lax.div(d, 4), lax.rem(d, 4))), 1)
    greet("atom", partner)

    loads = [
        pltpu.make_async_copy(src, dst, in_sem.at[k])
        for k, (src, dst) in enumerate(
            (
                (feat_in, feat), (species_in, species), (coords_in, coords), (embed_in, embed), (wc_in, w_charge_t),
                (widx_in, widx), (green_in, green), (wf_in, w_feat), (wp_in, w_pot), (wo_in, w_out),
            )
        )
    ]
    for load in loads:
        load.start()
    for load in loads[:5]:
        load.wait()

    hidden = feat[...].astype(F32)
    scale = lax.rsqrt(jnp.mean(hidden * hidden, axis=1, keepdims=True) + EPS)
    kinds = lax.broadcasted_iota(jnp.int32, (16, ATOMS), 0)
    onehot = (kinds == species[...]).astype(F32).astype(BF16)
    mixed_b = (hidden * scale + dot(onehot, embed[...], TN)).astype(BF16)
    mixed[...] = mixed_b
    cbuf[wave] = dot(w_charge_t[...], mixed_b, NT).astype(BF16)
    xbuf[wave] = coords[...]

    tmain[...] = jnp.zeros_like(tmain)
    tedge[...] = jnp.zeros_like(tedge)

    def prepare(slot, tabs, czs):
        place = xbuf[slot]
        for k in range(3):
            tabs[2 * k], tabs[2 * k + 1] = waves_of(place[k : k + 1])
        zcw, zsw = (tabs[k, pl.ds(wave, 1), :] for k in (4, 5))
        zbuf[slot] = jnp.concatenate([zcw, zsw, jnp.zeros((6, ATOMS), F32)], axis=0)
        wide = cbuf[slot].astype(F32)
        czs[...] = jnp.concatenate([zcw * wide, zsw * wide], axis=0).T.astype(BF16)

    def multiply(slot, tabs, czs):
        xc, xs, yc, ys = (tabs[k] for k in range(4))
        xcw, xsw, ycw, ysw = (tabs[k, pl.ds(wave, 1), :] for k in range(4))
        for i in range(N):
            a, b = xc[i : i + 1], xs[i : i + 1]
            for k, part in enumerate((a * yc, a * ys, b * yc, b * ys)):
                ebuf[slot, 64 * i + N * k : 64 * i + N * (k + 1), :] = part.astype(BF16)
        r = lax.broadcasted_iota(jnp.int32, (N, ATOMS), 0)
        one = jnp.where(r == 0, 1.0, 0.0)
        rest = jnp.zeros((N, ATOMS), F32)
        for k, row in enumerate((xcw, xsw, ycw, ysw)):
            rest = jnp.where(r == k + 1, row, rest)
        edge = (one, xc, xs, yc, ys, xcw * yc, xsw * ys, xsw * yc, xcw * ys, rest)
        for k, part in enumerate(edge):
            ebuf[slot, MAIN + N * k : MAIN + N * (k + 1), :] = part.astype(BF16)
        tmain[...] += dot(ebuf[slot, :LOW, :], czs[...])
        tedge[...] += dot(ebuf[slot, LOW:, :], cbuf[slot], NT)

    pl.semaphore_wait(barrier, 7 + 15 + 1)

    def c_copy(slot, peer):
        return push(cbuf.at[slot], cbuf.at[slot], send_sem.at[0], cr_sem.at[slot], "wave", peer)

    def x_copy(slot, peer):
        return push(xbuf.at[slot], xbuf.at[slot], send_sem.at[1], xr_sem.at[slot], "wave", peer)

    def send_on(slot, peer):
        x_copy(slot, peer).start()
        c_copy(slot, peer).start()

    for k in (1, 3, 0, 2, 4, 5, 6, 7):
        send_on(wave, at(PLACE_Y[k], PLACE_X[k]))

    for load in loads[5:]:
        load.wait()
    grid = green_rows(widx[0:1], widx[1:2], widx[2:3], green[...], atom)
    for k in range(N):
        gsend[k] = grid[8 * k : 8 * k + 8]
    gbuf[0] = gsend[wave]

    @functools.partial(times, N, start=1)
    def _(d):
        peer = at(lax.div(d, 4), lax.rem(d, 4))
        push(gsend.at[peer], gbuf.at[d], send_sem.at[2], gr_sem.at[0], "wave", peer).start()

    prepare(wave, tabs, czs)

    received = []
    for k in (1, 3, 0, 2, 4, 5, 6, 7, 9, 11, 8, 10, 12, 13, 14):
        code = PLACE_Y[k] + 4 * PLACE_X[k]
        if k < 6:
            code = code + 16 * STEP_Y[k] + 64 * STEP_X[k] + 256
        received.append(code)

    def receive(turn):
        code = pick(turn, received)
        slot = opposite(lax.rem(code, 4), lax.rem(lax.div(code, 4), 4))
        x_copy(slot, slot).wait_recv()
        c_copy(slot, slot).wait_recv()

        @pl.when(turn < 6)
        def _():
            send_on(slot, at(lax.rem(lax.div(code, 16), 4), lax.rem(lax.div(code, 64), 4)))

        @pl.when(turn == core)
        def _():
            send_on(slot, at(ahead, ahead))

        return slot

    def one(j, current):
        following = receive(j)
        for k in range(4):
            tabs_too[k] = tabs[k]
        multiply(current, tabs_too, czs)
        prepare(following, tabs, czs)
        return following

    current = lax.fori_loop(0, 15, one, wave)
    multiply(current, tabs, czs)

    wedge[0 : 4 * N, :] = tmain[MAIN + N : LOW, :]
    wedge[4 * N :, :] = jnp.concatenate([tedge[...], jnp.zeros((5 * N, Q), F32)], axis=1)
    wedge[8 * N : 8 * N + 8, :] += tmain[MAIN : MAIN + 8, :]

    def shard(i):
        main = tmain[pl.ds(pl.multiple_of(64 * i, 64), 64), :]
        return jnp.concatenate([main, wedge[pl.ds(i, 8, stride=N), :], wedge[8 * N : 8 * N + 8, :]], axis=0)

    for k in range(8):
        thalf[k] = shard(2 * k + 1 - core).astype(BF16)
    half_copy = push(thalf, tother, th_sem.at[0], th_sem.at[1], "atom", partner)
    half_copy.start()
    pre[...] = dot(mixed[...], w_feat[...])
    push(gsend.at[0:15], gbuf.at[1:16], send_sem.at[2], gr_sem.at[0], "wave", wave).wait_recv()
    gsum = gbuf[0]
    for k in range(1, N):
        gsum = gsum + gbuf[k]
    columns = jnp.concatenate([gsum, jnp.zeros((120, 128), F32)], axis=0).T

    half_copy.wait_recv()

    def t_copy(d):
        return push(tsend.at[d], trecv.at[d], send_sem.at[3], tr_sem.at[0], "atom", z_atom(d, core))

    for d in (4, 3, 5, 2, 6, 1, 7):
        owner = lax.rem(z + d, 8)
        tsend[d] = (shard(2 * owner + core) + tother[owner].astype(F32)).astype(BF16)
        t_copy(d).start()
    total = shard(atom) + tother[z].astype(F32)

    all_shards = push(tsend.at[1:8], trecv.at[1:8], send_sem.at[3], tr_sem.at[0], "atom", atom)
    all_shards.wait_recv()
    for d in range(1, 8):
        total = total + trecv[d].astype(F32)
    wall[atom] = apply_green(total, columns).astype(BF16)

    def w_copy(slot, peer):
        return push(wall.at[slot], wall.at[slot], send_sem.at[4], wr_sem.at[slot], "atom", peer)

    for d in (4, 3, 5, 2, 6, 1, 7):
        w_copy(atom, z_atom(d, core)).start()
    w_copy(atom, partner).start()
    wt[128:192, 0:MAIN] = jnp.zeros((64, MAIN), BF16)

    def place_pair(d):
        ring = lax.rem(z + 8 - d, 8)
        w_copy(2 * ring + 1 - core, partner).wait_recv()
        first, second = wall[2 * ring].astype(F32), wall[2 * ring + 1].astype(F32)
        pair = jnp.concatenate([first[0:64], second[0:64]], axis=0)
        wt[0:128, pl.ds(pl.multiple_of(128 * ring, 128), 128)] = pair.T.astype(BF16)
        wedge[pl.ds(2 * ring, 8, stride=N), :] = first[64:72]
        wedge[pl.ds(2 * ring + 1, 8, stride=N), :] = second[64:72]

    order = (0, 1, 7, 2, 6, 3, 5, 4)
    for j, d in enumerate(order):
        if d:
            source = z_atom(8 - d, core)
            w_copy(source, partner).wait_recv()
            w_copy(source, partner).start()
        if j >= 2:
            place_pair(order[j - 2])
    for d in order[-2:]:
        place_pair(d)
    tail = jnp.concatenate([wall[0, 72:80, :].astype(F32), jnp.zeros((8, 128), F32)], axis=0)
    edges = jnp.concatenate([tail, wedge[0 : 8 * N, :], tail, jnp.zeros((96, 128), F32)], axis=0)
    edges = jnp.concatenate([edges[:128].T, edges[128:].T], axis=1)
    column = lax.broadcasted_iota(jnp.int32, (128, 256), 1)
    low = jnp.where((column == 0) | ((column >= N) & (column < 5 * N)), edges, 0.0)
    high = jnp.where((column >= 5 * N) & (column != 9 * N), edges, 0.0)
    wt[0:128, MAIN:] = low[:, : ROWS - MAIN].astype(BF16)
    wt[128:192, MAIN:] = high[:Q, : ROWS - MAIN].astype(BF16)

    prelay[7] = jnp.zeros((Q, ATOMS), BF16)

    def partial(slot):
        u = dot(wt[...], ebuf[slot])
        v = zbuf[slot]
        return v[0:1] * u[0:Q] + v[1:2] * u[Q : 2 * Q] + u[2 * Q :]

    def up_copy(k, peer):
        return push(psend.at[k], precv.at[k], send_sem.at[5], pr_sem.at[k], "wave", peer)

    def relay_copy(k, r, peer):
        return push(psend.at[k], prelay.at[r], send_sem.at[5], pq_sem.at[r], "wave", peer)

    across = 4 - corner
    turns = (14, 8 + corner, 8, 10, 8 + across, 12, 13, 6, 7, 0, 2, corner, across, 4, 5)

    @functools.partial(times, 15)
    def _(j):
        k = pick(j, turns)
        slot = opposite(pick(k, PLACE_Y), pick(k, PLACE_X))
        value = partial(slot)

        @pl.when(k < 6)
        def _():
            relay_copy(0, k, slot).wait_recv()

        @pl.when(k == corner)
        def _():
            relay_copy(0, 6, slot).wait_recv()

        value = value + prelay[jnp.where(k < 6, k, 7)].astype(F32)
        value = value + prelay[jnp.where(k == corner, 6, 7)].astype(F32)
        psend[k] = value.astype(BF16)

        @pl.when(k < 8)
        def _():
            up_copy(k, slot).start()

        @pl.when(k >= 8)
        def _():
            step = k - 8
            relay_copy(k, step, opposite(pick(step, STEP_Y), pick(step, STEP_X))).start()

    potential = partial(wave)
    for k in (6, 7, 0, 2, 1, 3, 4, 5):
        up_copy(k, wave).wait_recv()
        potential = potential + precv[k].astype(F32)
    potential_b = potential.T.astype(BF16)
    before = pre[...] + dot(potential_b, w_pot[...])
    activation = (before / (1.0 + jnp.exp(-before))).astype(BF16)
    out[...] = (feat[...].astype(F32) + dot(activation, w_out[...])).astype(BF16)

    half_copy.wait_send()
    all_shards.wait_send()
    push(cbuf.at[0:15], cbuf.at[0:15], send_sem.at[0], cr_sem.at[0], "wave", wave).wait_send()
    push(xbuf.at[0:15], xbuf.at[0:15], send_sem.at[1], xr_sem.at[0], "wave", wave).wait_send()
    push(gsend.at[0:15], gbuf.at[1:16], send_sem.at[2], gr_sem.at[0], "wave", wave).wait_send()
    push(wall.at[0:15], wall.at[0:15], send_sem.at[4], wr_sem.at[0], "atom", atom).wait_send()
    push(psend, psend, send_sem.at[5], pr_sem.at[0], "wave", wave).wait_send()


def shards(features, species, coords, wave_index, green, embed, w_charge, w_feat, w_pot, w_out):
    operands = (
        features, species.reshape(1, -1), coords, wave_index, green.reshape(1, -1),
        embed, w_charge.T, w_feat, w_pot, w_out,
    )
    return pl.pallas_call(
        kernel,
        out_shape=pltpu.VMEM(features.shape, BF16),
        in_specs=[pl.BlockSpec(memory_space=pl.ANY)] * 10,
        out_specs=pl.BlockSpec(memory_space=pltpu.VMEM),
        scratch_shapes=[pltpu.VMEM(v.shape, v.dtype) for v in operands]
        + [
            pltpu.VMEM((N, Q, ATOMS), BF16),
            pltpu.VMEM((N, 3, ATOMS), F32),
            pltpu.VMEM((N, 8, 128), F32),
            pltpu.VMEM((N, 8, 128), F32),
            pltpu.VMEM((N, ROWS, ATOMS), BF16),
            pltpu.VMEM((N, 8, ATOMS), F32),
            pltpu.VMEM((6, N, ATOMS), F32),
            pltpu.VMEM((6, N, ATOMS), F32),
            pltpu.VMEM((ATOMS, 128), BF16),
            pltpu.VMEM((LOW, 128), F32),
            pltpu.VMEM((5 * N, Q), F32),
            pltpu.VMEM((9 * N, 128), F32),
            pltpu.VMEM((8, SHARD, 128), BF16),
            pltpu.VMEM((8, SHARD, 128), BF16),
            pltpu.VMEM((8, SHARD, 128), BF16),
            pltpu.VMEM((8, SHARD, 128), BF16),
            pltpu.VMEM((N, SHARD, 128), BF16),
            pltpu.VMEM((192, ROWS), BF16),
            pltpu.VMEM((15, Q, ATOMS), BF16),
            pltpu.VMEM((8, Q, ATOMS), BF16),
            pltpu.VMEM((8, Q, ATOMS), BF16),
            pltpu.VMEM((ATOMS, 128), BF16),
            pltpu.VMEM((ATOMS, 256), F32),
        ]
        + [pltpu.SemaphoreType.DMA((n,)) for n in (10, 6, N, N, 1, 2, 1, N, 8, 7)],
        compiler_params=pltpu.CompilerParams(
            collective_id=0, has_side_effects=True, vmem_limit_bytes=60 * 1024 * 1024
        ),
        name="ewald",
    )(*operands)


def solution(mesh):
    placed = (
        P(("atom", "wave"), None),
        P(("atom", "wave")),
        P(None, ("atom", "wave")),
        P(None, "wave"),
        P("wave"),
        P(),
        P(),
        P(),
        P(),
        P(),
    )
    return jax.shard_map(
        shards, mesh=mesh, in_specs=placed, out_specs=P(("atom", "wave"), None), check_vma=False
    )
```

time: 74.3 us -> 56 us (0.75)
  Pallas kernels: 71.1 us -> 55.3 us
  local copies, waits for them, and re-layouts: 3 us -> 0.66 us
    pallas_call x1, Pallas kernels: 71.1 us -> 55.3 us  [shards(): pl.pallas_call(kernel, out_shape=pltpu.VMEM(features.shape, BF16), in_spe...]
    unnamed x2 -> x1, local copies, waits for them, and re-layouts: 3 us -> 0.66 us
where the time goes in v2:
time: 56 us; the launch traced here: 55.9 us
  Pallas kernels  55.3 us (99%)
  local copies, waits for them, and re-layouts  0.66 us (1%)
    pallas_call x1, Pallas kernels, shards(): pl.pallas_call(kernel, out_shape=pltpu.VMEM(features.shape, BF16), in_spe...  55.3 us

profile of v2, /device:TPU:1, one launch (start us, length us, event | category | flops | bytes accessed | tf_op | source)
XLA Modules:
  0.0 55.9 jit_solution(9579322055636868030)
XLA Ops:
  0.0 55.3 %ewald.1 = bf16[512,128]{1,0:T(8,128)(2,1)S(1)} custom-call(bf16[512,128]{1,0:T(8,128)(2,1)} %feat_in.1, s32[1,512]{1,0:T(1,128)} %bitcast.5, f32[3,512]{1,0:T(4,128)} %coords_in.1, s32[3,1024]{1,0:T(4,128)} %widx_in.1, f32[1,1024]{1,0:T(1,128)} %bitcast.4, bf16[16,128]{1,0:T(8,128)(2,1)} %embed_in.1, bf16[64,128]{1,0:T(8,128)(2,1)} %bitcast.3, ...), custom_call_target="tpu_custom_call" | custom-call | tf_op jit(solution)/shard_map/ewald/pallas_call | solution.py:431
  55.3 0.7 %copy.12 = bf16[512,128]{1,0:T(8,128)(2,1)} copy(bf16[512,128]{1,0:T(8,128)(2,1)S(1)} %ewald.1) | data formatting | bytes 262144
